TPU v7x, 16 devices: a whole 2x2x2 slice. The times are simulated.
16 devices in a mesh: dp: 1, ep: 16 (over x, y, z, core).
Axes of the slice: x: 2, y: 2, z: 2, core: 2. Of those that a mesh axis runs over, the one named last changes fastest.
Arguments:
- x: bfloat16 [1, 16, 256, 1792], P('dp', 'ep')
- expert: int32 [1, 16, 256, 2], P('dp', 'ep')
- slot: int32 [1, 16, 256, 2], P('dp', 'ep')
- gate: float32 [1, 16, 256, 2], P('dp', 'ep')
- w_gate: bfloat16 [32, 1792, 4864], P('ep')
- w_up: bfloat16 [32, 1792, 4864], P('ep')
- w_down: bfloat16 [32, 4864, 1792], P('ep')
Outputs:
- y: bfloat16 [1, 16, 256, 1792], P('dp', 'ep')
All inputs are finite; a program needn't handle non-finite values.
Results may differ from a plain program's by a relative error of at most 0.009.
Values are sent between devices in bfloat16 or wider.
A program may use at most 2 GiB of HBM per device.

v0:
```python
import jax
import jax.numpy as jnp
from jax import lax
from jax.sharding import NamedSharding, PartitionSpec as P


def einsum(form, a, b):
    return jnp.einsum(form, a.astype(jnp.float32), b.astype(jnp.float32))


def solution(mesh):
    def placed(v, *spec):
        return lax.with_sharding_constraint(v, NamedSharding(mesh, P(*spec)))

    def step(x, expert, slot, gate, w_gate, w_up, w_down):
        experts, (tokens, top) = w_gate.shape[0], expert.shape[2:]
        slots = 5 * tokens * top // (4 * experts)
        to_expert = jax.nn.one_hot(expert, experts, dtype=jnp.bfloat16)
        to_slot = jax.nn.one_hot(slot, slots, dtype=jnp.bfloat16)
        weighted = to_expert * gate[..., None].astype(jnp.bfloat16)
        dispatch = einsum("abtke,abtkc->abtec", to_expert, to_slot).astype(jnp.bfloat16)
        combine = einsum("abtke,abtkc->abtec", weighted, to_slot).astype(jnp.bfloat16)
        z = einsum("abtec,abtd->aebcd", dispatch, x).astype(jnp.bfloat16)
        z = placed(z, "dp", None, "ep", None, None)
        z = placed(z, "dp", "ep", None, None, None)
        h = jax.nn.silu(einsum("aebcd,edf->aebcf", z, w_gate))
        h = (h * einsum("aebcd,edf->aebcf", z, w_up)).astype(jnp.bfloat16)
        out = einsum("aebcf,efd->aebcd", h, w_down).astype(jnp.bfloat16)
        out = placed(out, "dp", "ep", None, None, None)
        out = placed(out, "dp", None, "ep", None, None)
        y = einsum("abtec,aebcd->abtd", combine, out)
        return y.astype(jnp.bfloat16)

    return step
```

profile of v0, /device:TPU:0, one launch (start us, length us, event | category | flops | bytes accessed | tf_op | source)
XLA Modules:
  0.0 170.7 jit_solution(10563939836767673383)
XLA Ops:
  0.0 0.0 copy-start
  0.0 0.9 copy.11
  0.9 0.0 copy-start.2
  0.9 0.8 copy.9
  1.8 0.0 copy-done.2
  1.8 0.0 copy-start.4
  1.8 0.7 copy-done.4
  2.4 2.8 %convolution_convert_fusion.1 = bf16[256,32,20]{1,2,0:T(8,128)(2,1)S(1)} fusion(s32[256,2]{1,0:T(8,128)S(1)} %copy.11, s32[256,2]{1,0:T(8,128)S(1)} %copy.9), kind=kOutput, calls=%fused_computation.26 | convolution fusion | flops 845824 | bytes 331776 | tf_op jit(solution)/abtke,abtkc->abtec/dot_general | solution.py:8
  5.2 0.0 copy-done
  5.2 1.1 fusion.28
  6.3 2.3 %reshape.52 = bf16[1,16,2,1,20,1792]{5,2,1,4,3,0:T(2,128)(2,1)} reshape(bf16[1,32,1,20,1792]{4,1,3,2,0:T(8,128)(2,1)S(1)} %fusion.28) | data formatting | bytes 4587520 | tf_op jit(solution)/sharding_constraint;jit(solution)/sharding_constraint | solution.py:13
  8.6 3.2 %copy.13 = bf16[1,16,2,1,20,1792]{5,2,4,3,0,1:T(2,128)(2,1)S(1)} copy(bf16[1,16,2,1,20,1792]{5,2,1,4,3,0:T(2,128)(2,1)} %reshape.52) | data formatting | bytes 4587520 | tf_op jit(solution)/sharding_constraint;jit(solution)/sharding_constraint | solution.py:13
  11.9 34.6 %all-to-all.4 = bf16[1,16,2,1,20,1792]{5,2,4,3,0,1:T(2,128)(2,1)S(1)} all-to-all(bf16[1,16,2,1,20,1792]{5,2,4,3,0,1:T(2,128)(2,1)S(1)} %copy.13), channel_id=1, replica_groups=mesh['dp'=1,'ep'=16] {'ep'}, dimensions={1} | all-to-all | bytes 4587520 | tf_op jit(solution)/sharding_constraint;jit(solution)/sharding_constraint | solution.py:13
  46.4 23.1 %fusion.4 = f32[2,16,20,4864]{3,2,1,0:T(8,128)} fusion(bf16[2,1792,4864]{2,1,0:T(8,128)(2,1)} %param.4, bf16[1,16,2,1,20,1792]{5,2,4,3,0,1:T(2,128)(2,1)S(1)} %all-to-all.4), kind=kOutput, calls=%fused_computation.4 | convolution fusion | flops 11156848640 | bytes 49610752 | tf_op jit(solution)/aebcd,edf->aebcf/dot_general | solution.py:8
  69.5 27.6 %fusion.12.clone.8 = bf16[2,16,20,4864]{3,2,1,0:T(8,128)(2,1)} fusion(bf16[2,1792,4864]{2,1,0:T(8,128)(2,1)} %param.5, f32[2,16,20,4864]{3,2,1,0:T(8,128)} %fusion.4, bf16[1,16,2,1,20,1792]{5,2,4,3,0,1:T(2,128)(2,1)S(1)} %all-to-all.4), kind=kOutput, calls=%fused_computation.13.clone.clone.clone.clone.clone.clone.clone.1 | convolution fusion | flops 11175526400 | bytes 55836672 | tf_op jit(solution)/aebcd,edf->aebcf/dot_general | solution.py:8
  97.1 22.1 %fusion.23 = bf16[1,2,16,1,20,1792]{5,4,2,1,3,0:T(8,128)(2,1)} fusion(bf16[2,4864,1792]{2,1,0:T(8,128)(2,1)} %param.6, bf16[2,16,20,4864]{3,2,1,0:T(8,128)(2,1)} %fusion.12.clone.8), kind=kOutput, calls=%fused_computation.17 | convolution fusion | flops 11157995520 | bytes 43384832 | tf_op jit(solution)/aebcf,efd->aebcd/dot_general | solution.py:8
  119.2 5.6 %copy.15 = bf16[1,2,16,1,20,1792]{5,1,4,3,0,2:T(2,128)(2,1)} copy(bf16[1,2,16,1,20,1792]{5,4,2,1,3,0:T(8,128)(2,1)} %fusion.23) | data formatting | bytes 4587520 | tf_op jit(solution)/sharding_constraint;jit(solution)/sharding_constraint | solution.py:13
  124.8 0.0 copy-start.6
  124.8 0.0 copy-start.3
  124.8 0.0 copy-start.5
  124.8 2.9 %all-to-all-start.1 = ((bf16[1,2,16,1,20,1792]{5,1,4,3,0,2:T(2,128)(2,1)}), bf16[1,2,16,1,20,1792]{5,1,4,3,0,2:T(2,128)(2,1)S(1)}, u32[]{:S(2)}, u32[]{:S(2)}) async-start(bf16[1,2,16,1,20,1792]{5,1,4,3,0,2:T(2,128)(2,1)} %copy.15), calls=%async_computation.1 | async-start | bytes 4587520 | tf_op jit(solution)/sharding_constraint;jit(solution)/sharding_constraint | solution.py:13
  127.6 0.0 copy-done.6
  127.6 0.1 copy.10
  127.8 0.0 copy-done.3
  127.8 0.0 copy-done.5
  127.8 3.9 %convolution_convert_fusion.2 = bf16[256,32,20]{1,2,0:T(8,128)(2,1)} fusion(s32[256,2]{1,0:T(8,128)S(1)} %copy-done.3, s32[256,2]{1,0:T(8,128)S(1)} %copy-done.5, bf16[256,2]{1,0:T(8,128)(2,1)S(1)} %copy.10), kind=kOutput, calls=%fused_computation.27 | convolution fusion | flops 862208 | bytes 332800 | tf_op jit(solution)/abtke,abtkc->abtec/dot_general | solution.py:8
  131.7 26.7 %all-to-all-done.1 = bf16[1,2,16,1,20,1792]{5,1,4,3,0,2:T(2,128)(2,1)S(1)} async-done(((bf16[1,2,16,1,20,1792]{5,1,4,3,0,2:T(2,128)(2,1)}), bf16[1,2,16,1,20,1792]{5,1,4,3,0,2:T(2,128)(2,1)S(1)}, u32[]{:S(2)}, u32[]{:S(2)}) %all-to-all-start.1) | async-done | bytes 2293792 | tf_op jit(solution)/sharding_constraint;jit(solution)/sharding_constraint | solution.py:13
  158.4 3.7 %copy.16 = bf16[1,16,2,1,20,1792]{5,2,1,4,3,0:T(2,128)(2,1)} copy(bf16[1,16,2,1,20,1792]{5,2,4,3,0,1:T(2,128)(2,1)S(1)} %bitcast.156) | data formatting | bytes 4587520 | tf_op jit(solution)/sharding_constraint;jit(solution)/sharding_constraint | solution.py:13
  162.1 4.8 %reshape.77 = bf16[32,20,1792]{2,0,1:T(8,128)(2,1)S(1)} reshape(bf16[1,16,2,1,20,1792]{5,2,1,4,3,0:T(2,128)(2,1)} %copy.16) | data formatting | bytes 4587520
  167.0 0.0 copy-start.1
  167.0 3.6 %fusion.36 = bf16[1,1,256,1792]{3,2,1,0:T(8,128)(2,1)} fusion(bf16[32,20,1792]{2,0,1:T(8,128)(2,1)S(1)} %reshape.77, bf16[256,32,20]{1,2,0:T(8,128)(2,1)} %convolution_convert_fusion.2), kind=kOutput, calls=%fused_computation.25 | convolution fusion | flops 587661312 | bytes 3538944 | tf_op jit(solution)/abtec,aebcd->abtd/dot_general | solution.py:8
  170.7 0.0 copy-done.1
  (1 shorter events, 0.0 us)
Async XLA Ops:
  0.0 5.2 %copy-start = (bf16[1,1,256,1792]{3,2,1,0:T(8,128)(2,1)S(1)}, bf16[1,1,256,1792]{3,2,1,0:T(8,128)(2,1)}, u32[]{:S(2)}) copy-start(bf16[1,1,256,1792]{3,2,1,0:T(8,128)(2,1)} %param.3) | copy-start | bytes 2752516
  0.9 0.9 copy-start.2
  1.8 0.7 copy-start.4
  124.8 2.9 %copy-start.6 = (f32[1,1,256,2]{2,3,1,0:T(2,128)S(1)}, f32[1,1,256,2]{2,3,1,0:T(2,128)}, u32[]{:S(2)}) copy-start(f32[1,1,256,2]{2,3,1,0:T(2,128)} %param.1) | copy-start | bytes 6148
  124.8 3.0 %copy-start.3 = (s32[256,2]{1,0:T(8,128)S(1)}, s32[256,2]{1,0:T(8,128)}, u32[]{:S(2)}) copy-start(s32[256,2]{1,0:T(8,128)} %copy-done.2) | copy-start | bytes 6148
  124.8 3.0 %copy-start.5 = (s32[256,2]{1,0:T(8,128)S(1)}, s32[256,2]{1,0:T(8,128)}, u32[]{:S(2)}) copy-start(s32[256,2]{1,0:T(8,128)} %copy-done.4) | copy-start | bytes 6148
  124.8 33.7 %all-to-all-start.1 = ((bf16[1,2,16,1,20,1792]{5,1,4,3,0,2:T(2,128)(2,1)}), bf16[1,2,16,1,20,1792]{5,1,4,3,0,2:T(2,128)(2,1)S(1)}, u32[]{:S(2)}, u32[]{:S(2)}) async-start(bf16[1,2,16,1,20,1792]{5,1,4,3,0,2:T(2,128)(2,1)} %copy.15), calls=%async_computation.1 | async-start | bytes 4587520 | tf_op jit(solution)/sharding_constraint;jit(solution)/sharding_constraint | solution.py:13
  167.0 3.7 %copy-start.1 = (bf16[1,1,256,1792]{3,2,1,0:T(8,128)(2,1)S(1)}, bf16[1,1,256,1792]{3,2,1,0:T(8,128)(2,1)}, u32[]{:S(2)}) copy-start(bf16[1,1,256,1792]{3,2,1,0:T(8,128)(2,1)} %param.3) | copy-start | bytes 2752516
where the time goes:
time: 171 us
  matrix products  84.2 us (49%)
  blocking collectives  34.6 us (20%)
  waiting for transfers between devices  26.7 us (16%)
  local copies, waits for them, and re-layouts  22.2 us (13%)
  starting transfers between devices  2.85 us (2%)
    dot_general x7, matrix products, einsum(): return jnp.einsum(form, a.astype(jnp.float32), b.astype(jnp.float32))  84.2 us
    another operation x1, blocking collectives, placed(): return lax.with_sharding_constraint(v, NamedSharding(mesh, P(*spec)))  34.6 us
    another operation x1, waiting for transfers between devices, placed(): return lax.with_sharding_constraint(v, NamedSharding(mesh, P(*spec)))  26.7 us
    another operation x4, local copies, waits for them, and re-layouts, placed(): return lax.with_sharding_constraint(v, NamedSharding(mesh, P(*spec)))  14.8 us
    unnamed x15, local copies, waits for them, and re-layouts  5.53 us
  transfers between devices with their start and end apart: 1, of which 1 were waited for; matrix products, arithmetic and copies ran while one was open for 2% of the time, Pallas kernels for 0%

commit v1 on v0

v1 whole, which is shorter than its diff:
```python
import functools

import jax
import jax.numpy as jnp
from jax import lax
from jax.experimental import pallas as pl
from jax.experimental.pallas import tpu as pltpu
from jax.sharding import PartitionSpec as P

N = 16
LOCAL = 2
T, D, F = 256, 1792, 4864
SLOTS, MAIN = 20, 16
HALF = D // 2
FT = 256
NF = F // FT
RING = 8
CHUNKS = ((0, 512), (512, 512), (1024, 512), (1536, 256))
f32, bf16, i32 = jnp.float32, jnp.bfloat16, jnp.int32


def dot(a, b):
    return jnp.dot(a, b, preferred_element_type=f32)


def iota(shape, axis):
    return lax.broadcasted_iota(i32, shape, axis)


def kernel(x_hbm, expert, slot, gate, wg_hbm, wu_hbm, wd_hbm, y_ref,
           x_v, zs, zr, lhs, h, wb, wd, os0, os1, os2, os3, cr0, cr1, cr2, cr3,
           x_sem, wb_sem, wd_sem, ds_sem, dr_sem, cs_sem, cr_sem):
    os, cr = (os0, os1, os2, os3), (cr0, cr1, cr2, cr3)
    me = lax.axis_index("ep")
    bits = [(me // (1 << b)) % 2 for b in range(4)]

    def partner(k):
        return sum((1 - bits[b] if (k >> b) & 1 else bits[b]) * (1 << b) for b in range(4))

    order = [partner((7 * k) % 16) for k in range(1, N)]

    x_copy = pltpu.make_async_copy(x_hbm, x_v, x_sem)
    x_copy.start()
    barrier = pltpu.get_barrier_semaphore()
    for d in order:
        pl.semaphore_signal(barrier, inc=1, device_id={"ep": d}, device_id_type=pl.DeviceIdType.MESH)

    def wb_copies(g):
        e, f, s = g // NF, g % NF, g % RING
        cols = pl.ds(pl.multiple_of(f * FT, FT), FT)
        return (pltpu.make_async_copy(wg_hbm.at[e, :, cols], wb.at[s, :, pl.ds(0, FT)], wb_sem.at[s]),
                pltpu.make_async_copy(wu_hbm.at[e, :, cols], wb.at[s, :, pl.ds(FT, FT)], wb_sem.at[s]))

    def wd_copy(e, c):
        cols = pl.ds(*CHUNKS[c])
        return pltpu.make_async_copy(wd_hbm.at[e, :, cols], wd.at[:, cols], wd_sem.at[c])

    col = [jnp.where(slot[:, j:j + 1] < SLOTS, expert[:, j:j + 1] * 32 + slot[:, j:j + 1], -1) for j in range(2)]
    row = [jnp.transpose(jnp.broadcast_to(c, (T, 128)))[0:1, :] for c in col]
    weight = [gate[:, j:j + 1].astype(bf16).astype(f32) for j in range(2)]

    def main_code(r, e):
        return (2 * (r >> 4) + e) * 32 + (r & 15)

    def rem_code(r, e, side):
        return jnp.where(((r >> 2) & 1) == side, (2 * (r >> 3) + e) * 32 + MAIN + (r & 3), -2)

    def pick(code):
        shape = (code.shape[0], T)
        hit = (jnp.broadcast_to(code, shape) == jnp.broadcast_to(row[0], shape)) | (
            jnp.broadcast_to(code, shape) == jnp.broadcast_to(row[1], shape))
        return jnp.where(hit, 1.0, 0.0).astype(bf16)

    def blend(code):
        shape = (T, code.shape[1])
        return sum(jnp.where(jnp.broadcast_to(col[j], shape) == jnp.broadcast_to(code, shape),
                             jnp.broadcast_to(weight[j], shape), 0.0) for j in range(2)).astype(bf16)

    x_copy.wait()
    for g in range(RING):
        for c in wb_copies(g):
            c.start()
    for c in range(len(CHUNKS)):
        wd_copy(0, c).start()

    def disp(e, d):
        return pltpu.make_async_remote_copy(
            src_ref=zs.at[e, d], dst_ref=zr.at[e, me], send_sem=ds_sem.at[e], recv_sem=dr_sem.at[e],
            device_id={"ep": d}, device_id_type=pl.DeviceIdType.MESH)

    for e in range(LOCAL):
        z = dot(pick(main_code(iota((N * MAIN, 1), 0), e)), x_v[...]).astype(bf16)
        zs[e, :, 0:16, :] = z[:, :HALF].reshape(N, 16, HALF)
        zs[e, :, 16:32, :] = z[:, HALF:].reshape(N, 16, HALF)
        r = iota((N * 8, 1), 0)
        z = dot(pick(rem_code(r, e, 0)), x_v[:, :HALF]) + dot(pick(rem_code(r, e, 1)), x_v[:, HALF:])
        zs[e, :, 32:40, :] = z.astype(bf16).reshape(N, 8, HALF)
        if e == 0:
            pl.semaphore_wait(barrier, N - 1)
        for d in order:
            disp(e, d).start()
        zr[e, me] = zs[e, me]

    fold_l = jnp.where(((iota((128, 64), 0) >> 3) * 4 + (iota((128, 64), 0) & 7)) == iota((128, 64), 1), 1.0, 0.0)
    fold_l = jnp.where((iota((128, 64), 0) & 7) < 4, fold_l, 0.0).astype(bf16)
    fold_r = jnp.where(((iota((128, 64), 0) >> 3) * 4 + (iota((128, 64), 0) & 7) - 4) == iota((128, 64), 1), 1.0, 0.0)
    fold_r = jnp.where((iota((128, 64), 0) & 7) >= 4, fold_r, 0.0).astype(bf16)
    un_r = iota((64, 128), 0)
    un_c = iota((64, 128), 1)
    unfold_l = jnp.where((un_r >> 2) * 8 + (un_r & 3) == un_c, 1.0, 0.0).astype(bf16)
    unfold_r = jnp.where((un_r >> 2) * 8 + (un_r & 3) + 4 == un_c, 1.0, 0.0).astype(bf16)

    def comb(e, c, d):
        return pltpu.make_async_remote_copy(
            src_ref=os[c].at[e, d], dst_ref=cr[c].at[e, me], send_sem=cs_sem.at[e, c], recv_sem=cr_sem.at[e, c],
            device_id={"ep": d}, device_id_type=pl.DeviceIdType.MESH)

    def landed(ref, sem):
        pltpu.make_async_copy(ref.at[pl.ds(0, N - 1)], ref.at[pl.ds(0, N - 1)], sem).wait()

    for e in range(LOCAL):
        landed(zr.at[e], dr_sem.at[e])
        lhs[0:256, :HALF] = zr[e, :, 0:16, :].reshape(N * 16, HALF)
        lhs[0:256, HALF:] = zr[e, :, 16:32, :].reshape(N * 16, HALF)
        rem = zr[e, :, 32:40, :].reshape(N * 8, HALF)
        lhs[256:320, :HALF] = dot(unfold_l, rem).astype(bf16)
        lhs[256:320, HALF:] = dot(unfold_r, rem).astype(bf16)

        @pl.loop(0, NF)
        def _(f):
            g = e * NF + f
            s = g % RING
            pltpu.make_async_copy(wb.at[s], wb.at[s], wb_sem.at[s]).wait()
            gu = dot(lhs[...], wb[s])
            h[:, pl.ds(pl.multiple_of(f * FT, FT), FT)] = (jax.nn.silu(gu[:, :FT]) * gu[:, FT:]).astype(bf16)

            @pl.when(g + RING < LOCAL * NF)
            def _():
                for c in wb_copies(g + RING):
                    c.start()

        for c, (c0, width) in enumerate(CHUNKS):
            w2 = width // 2
            wd_copy(e, c).wait()
            out = dot(h[...], wd[:, pl.ds(c0, width)]).astype(bf16)
            if e + 1 < LOCAL:
                wd_copy(e + 1, c).start()
            os[c][e, :, 0:16, :] = out[0:256, :w2].reshape(N, 16, w2)
            os[c][e, :, 16:32, :] = out[0:256, w2:].reshape(N, 16, w2)
            rem = dot(fold_l, out[256:320, :w2]) + dot(fold_r, out[256:320, w2:])
            os[c][e, :, 32:40, :] = rem.astype(bf16).reshape(N, 8, w2)
            for d in order:
                comb(e, c, d).start()
            cr[c][e, me] = os[c][e, me]

    mains = [blend(main_code(iota((1, 256), 1), e)) for e in range(LOCAL)]
    rems = [[blend(rem_code(iota((1, 128), 1), e, side)) for side in range(2)] for e in range(LOCAL)]
    for c, (c0, width) in enumerate(CHUNKS):
        w2 = width // 2
        for e in range(LOCAL):
            landed(cr[c].at[e], cr_sem.at[e, c])
        for side in range(2):
            acc = 0
            for e in range(LOCAL):
                acc += dot(mains[e], cr[c][e, :, 16 * side:16 * side + 16, :].reshape(N * 16, w2))
                acc += dot(rems[e][side], cr[c][e, :, 32:40, :].reshape(N * 8, w2))
            y_ref[:, pl.ds(c0 + side * w2, w2)] = acc.astype(bf16)

    for e in range(LOCAL):
        landed(zs.at[e], ds_sem.at[e])
        for c in range(len(CHUNKS)):
            landed(os[c].at[e], cs_sem.at[e, c])


def solution(mesh):
    def body(x, expert, slot, gate, wg, wu, wd):
        vmem = pl.BlockSpec(memory_space=pltpu.VMEM)
        hbm = pl.BlockSpec(memory_space=pltpu.HBM)
        halves = [w // 2 for _, w in CHUNKS]
        y = pl.pallas_call(
            kernel,
            name="moe",
            out_shape=jax.ShapeDtypeStruct((T, D), bf16),
            in_specs=[hbm, vmem, vmem, vmem, hbm, hbm, hbm],
            out_specs=vmem,
            scratch_shapes=[
                pltpu.VMEM((T, D), bf16),
                pltpu.VMEM((LOCAL, N, 40, HALF), bf16),
                pltpu.VMEM((LOCAL, N, 40, HALF), bf16),
                pltpu.VMEM((N * SLOTS, D), bf16),
                pltpu.VMEM((N * SLOTS, F), bf16),
                pltpu.VMEM((RING, D, 2 * FT), bf16),
                pltpu.VMEM((F, D), bf16),
                *[pltpu.VMEM((LOCAL, N, 40, w), bf16) for w in halves],
                *[pltpu.VMEM((LOCAL, N, 40, w), bf16) for w in halves],
                pltpu.SemaphoreType.DMA,
                pltpu.SemaphoreType.DMA((RING,)),
                pltpu.SemaphoreType.DMA((len(CHUNKS),)),
                pltpu.SemaphoreType.DMA((LOCAL,)),
                pltpu.SemaphoreType.DMA((LOCAL,)),
                pltpu.SemaphoreType.DMA((LOCAL, len(CHUNKS))),
                pltpu.SemaphoreType.DMA((LOCAL, len(CHUNKS))),
            ],
            compiler_params=pltpu.CompilerParams(
                collective_id=0, has_side_effects=True, vmem_limit_bytes=67_000_000),
        )(x[0, 0], expert[0, 0], slot[0, 0], gate[0, 0], wg, wu, wd)
        return y[None, None]

    tok, weights = P("dp", "ep", None, None), P("ep", None, None)
    return jax.shard_map(body, mesh=mesh, in_specs=(tok,) * 4 + (weights,) * 3, out_specs=tok, check_vma=False)
```

time: 171 us -> 86.2 us (0.50)
  matrix products: 84.2 us -> 0 us
  Pallas kernels: 0 us -> 79.3 us
  blocking collectives: 34.6 us -> 0 us
  waiting for transfers between devices: 26.7 us -> 0 us
  local copies, waits for them, and re-layouts: 22.2 us -> 6.58 us
  starting transfers between devices: 2.85 us -> 0 us
    dot_general x7 -> x0, matrix products: 84.2 us -> none  [einsum(): return jnp.einsum(form, a.astype(jnp.float32), b.astype(jnp.float32))]
    pallas_call x0 -> x1, Pallas kernels: none -> 79.3 us  [body(): pl.pallas_call(kernel, name='moe', out_shape=jax.ShapeDtypeStruct((T, D),...]
    another operation x1 -> x0, blocking collectives: 34.6 us -> none  [placed(): return lax.with_sharding_constraint(v, NamedSharding(mesh, P(*spec)))]
    another operation x1 -> x0, waiting for transfers between devices: 26.7 us -> none  [placed(): return lax.with_sharding_constraint(v, NamedSharding(mesh, P(*spec)))]
    another operation x4 -> x0, local copies, waits for them, and re-layouts: 14.8 us -> none  [placed(): return lax.with_sharding_constraint(v, NamedSharding(mesh, P(*spec)))]
    another operation x1 -> x0, starting transfers between devices: 2.85 us -> none  [placed(): return lax.with_sharding_constraint(v, NamedSharding(mesh, P(*spec)))]
    eq x2 -> x0, local copies, waits for them, and re-layouts: 1.72 us -> none  [the longest x1 0.89 us: step(): to_slot = jax.nn.one_hot(slot, slots, dtype=jnp.bfloat16)]
    unnamed x15 -> x4, local copies, waits for them, and re-layouts: 5.53 us -> 6.58 us
  transfers between devices with their start and end apart: 1 -> 0, of which waited for: 1 -> 0; matrix products, arithmetic and copies ran while one was open for 2% -> 0% of each run, Pallas kernels for 0% -> 0%
where the time goes in v1:
time: 86.2 us; the launch traced here: 85.9 us
  Pallas kernels  79.3 us (92%)
  local copies, waits for them, and re-layouts  6.58 us (8%)
    pallas_call x1, Pallas kernels, body(): pl.pallas_call(kernel, name='moe', out_shape=jax.ShapeDtypeStruct((T, D),...  79.3 us
    unnamed x4, local copies, waits for them, and re-layouts  6.58 us

profile of v1, /device:TPU:0, one launch (start us, length us, event | category | flops | bytes accessed | tf_op | source)
XLA Modules:
  0.0 85.9 jit_solution(17463300298143692006)
XLA Ops:
  0.0 1.5 %copy.8 = s32[1,1,256,2]{3,2,1,0:T(8,128)} copy(s32[1,1,256,2]{2,3,1,0:T(2,128)} %param.8) | data formatting | bytes 4096 | tf_op args[1]
  1.5 1.5 %copy.9 = s32[1,1,256,2]{3,2,1,0:T(8,128)} copy(s32[1,1,256,2]{2,3,1,0:T(2,128)} %param.9) | data formatting | bytes 4096 | tf_op args[2]
  3.0 1.5 %copy.10 = f32[1,1,256,2]{3,2,1,0:T(8,128)} copy(f32[1,1,256,2]{2,3,1,0:T(2,128)} %param.10) | data formatting | bytes 4096 | tf_op args[3]
  4.4 79.3 %moe.1 = bf16[256,1792]{1,0:T(8,128)(2,1)} custom-call(bf16[256,1792]{1,0:T(8,128)(2,1)} %bitcast.6, s32[256,2]{1,0:T(8,128)} %bitcast.7, s32[256,2]{1,0:T(8,128)} %bitcast.8, f32[256,2]{1,0:T(8,128)} %bitcast.9, bf16[2,1792,4864]{2,1,0:T(8,128)(2,1)} %wg_hbm.1, bf16[2,1792,4864]{2,1,0:T(8,128)(2,1)} %wu_hbm.1, bf16[2,4864,1792]{2,1,0:T(8,128)(2,1)} %wd_hbm.1), custom_call_target="tpu_custom_call" | custom-call | tf_op jit(solution)/shard_map/moe/pallas_call | solution.py:180
  83.7 2.2 %copy.12 = bf16[1,1,256,1792]{3,2,1,0:T(8,128)(2,1)} copy(bf16[1,1,256,1792]{3,2,1,0:T(8,128)(2,1)} %bitcast.5) | data formatting | bytes 1835008

commit v2 on v1

v2 whole, which is shorter than its diff:
```python
import functools

import jax
import jax.numpy as jnp
from jax import lax
from jax.experimental import pallas as pl
from jax.experimental.pallas import tpu as pltpu
from jax.sharding import PartitionSpec as P

N = 16
LOCAL = 2
VMEM_LIMIT = 65_500_000
T, D, F = 256, 1792, 4864
SLOTS, MAIN = 20, 16
KS = ((0, 1024), (1024, 768))
FT = 256
NF = F // FT
RING, GROUP = 8, 4
CHUNKS = ((0, 512), (512, 512), (1024, 512), (1536, 256))
f32, bf16, i32 = jnp.float32, jnp.bfloat16, jnp.int32


def dot(a, b):
    return jnp.dot(a, b, preferred_element_type=f32)


def iota(shape, axis):
    return lax.broadcasted_iota(i32, shape, axis)


def kernel(x_hbm, expert, slot, gate, wg_hbm, wu_hbm, wd_hbm, y_ref,
           x_v, zs0, zs1, zr0, zr1, lhs, acc, h, wb, wd, os0, os1, os2, os3, cr0, cr1, cr2, cr3, bm, br,
           x_sem, wb_sem, wd_sem, ds_sem, dr_sem, cs_sem, cr_sem):
    zs, zr = (zs0, zs1), (zr0, zr1)
    os, cr = (os0, os1, os2, os3), (cr0, cr1, cr2, cr3)
    me = lax.axis_index("ep")
    bits = [(me // (1 << b)) % 2 for b in range(4)]

    def partner(k):
        return sum((1 - bits[b] if (k >> b) & 1 else bits[b]) * (1 << b) for b in range(4))

    order = [partner((7 * k) % 16) for k in range(1, N)]

    x_copy = pltpu.make_async_copy(x_hbm, x_v, x_sem)
    x_copy.start()
    barrier = pltpu.get_barrier_semaphore()
    for d in order:
        pl.semaphore_signal(barrier, inc=1, device_id={"ep": d}, device_id_type=pl.DeviceIdType.MESH)

    def wb_start(g, k):
        e, f, s = g // NF, g % NF, g % RING
        rows, cols = pl.ds(*KS[k]), pl.ds(pl.multiple_of(f * FT, FT), FT)
        pltpu.make_async_copy(wg_hbm.at[e, rows, cols], wb.at[s, rows, pl.ds(0, FT)], wb_sem.at[k, s]).start()
        pltpu.make_async_copy(wu_hbm.at[e, rows, cols], wb.at[s, rows, pl.ds(FT, FT)], wb_sem.at[k, s]).start()

    def wb_wait(g, k):
        part = wb.at[g % RING, pl.ds(*KS[k])]
        pltpu.make_async_copy(part, part, wb_sem.at[k, g % RING]).wait()

    def wd_copy(e, c):
        cols = pl.ds(*CHUNKS[c])
        return pltpu.make_async_copy(wd_hbm.at[e, :, cols], wd.at[:, cols], wd_sem.at[c])

    row = [jnp.where(slot[j:j + 1] < SLOTS, expert[j:j + 1] * 32 + slot[j:j + 1], -1) for j in range(2)]

    def main_code(r, e):
        return (2 * (r >> 4) + e) * 32 + (r & 15)

    def rem_code(r, e, side):
        return jnp.where(((r >> 2) & 1) == side, (2 * (r >> 3) + e) * 32 + MAIN + (r & 3), -2)

    def pick(code):
        shape = (code.shape[0], T)
        hit = (jnp.broadcast_to(code, shape) == jnp.broadcast_to(row[0], shape)) | (
            jnp.broadcast_to(code, shape) == jnp.broadcast_to(row[1], shape))
        return jnp.where(hit, 1.0, 0.0).astype(bf16)

    def column(v):
        return jnp.transpose(jnp.broadcast_to(v, (128, T)))[:, 0:1]

    def disp(e, k, d):
        return pltpu.make_async_remote_copy(
            src_ref=zs[k].at[e, d], dst_ref=zr[k].at[e, me], send_sem=ds_sem.at[e, k], recv_sem=dr_sem.at[e, k],
            device_id={"ep": d}, device_id_type=pl.DeviceIdType.MESH)

    def gather(e, k, mains, rems):
        k0, width = KS[k]
        w2 = width // 2
        z = dot(mains, x_v[:, pl.ds(k0, width)]).astype(bf16)
        zs[k][e, :, 0:16, :] = z[:, :w2].reshape(N, 16, w2)
        zs[k][e, :, 16:32, :] = z[:, w2:].reshape(N, 16, w2)
        z = dot(rems[0], x_v[:, pl.ds(k0, w2)]) + dot(rems[1], x_v[:, pl.ds(k0 + w2, w2)])
        zs[k][e, :, 32:40, :] = z.astype(bf16).reshape(N, 8, w2)

    for e in range(LOCAL):
        r = iota((N * 8, 1), 0)
        mains = pick(main_code(iota((N * MAIN, 1), 0), e))
        rems = [pick(rem_code(r, e, side)) for side in range(2)]
        if e == 0:
            x_copy.wait()
        for k in range(len(KS)):
            gather(e, k, mains, rems)
            if e == 0 and k == 0:
                pl.semaphore_wait(barrier, N - 1)
            for d in order:
                disp(e, k, d).start()
            zr[k][e, me] = zs[k][e, me]
            if e == 0:
                for g in range(RING):
                    wb_start(g, k)
    for c in range(len(CHUNKS)):
        wd_copy(0, c).start()

    un_r = iota((64, 128), 0)
    un_c = iota((64, 128), 1)
    unfold_l = jnp.where((un_r >> 2) * 8 + (un_r & 3) == un_c, 1.0, 0.0).astype(bf16)
    unfold_r = jnp.where((un_r >> 2) * 8 + (un_r & 3) + 4 == un_c, 1.0, 0.0).astype(bf16)

    col = [column(row[j]) for j in range(2)]
    weight = [column(gate[j:j + 1].astype(bf16).astype(f32)) for j in range(2)]

    def blend(code):
        shape = (T, code.shape[1])
        return sum(jnp.where(jnp.broadcast_to(col[j], shape) == jnp.broadcast_to(code, shape),
                             jnp.broadcast_to(weight[j], shape), 0.0) for j in range(2)).astype(bf16)

    for e in range(LOCAL):
        bm[e] = blend(main_code(iota((1, 256), 1), e))
        for side in range(2):
            br[e, side] = blend(rem_code(iota((1, 128), 1), e, side))

    def comb(e, c, d):
        return pltpu.make_async_remote_copy(
            src_ref=os[c].at[e, d], dst_ref=cr[c].at[e, me], send_sem=cs_sem.at[e, c], recv_sem=cr_sem.at[e, c],
            device_id={"ep": d}, device_id_type=pl.DeviceIdType.MESH)

    def landed(ref, sem):
        pltpu.make_async_copy(ref.at[pl.ds(0, N - 1)], ref.at[pl.ds(0, N - 1)], sem).wait()

    def arrive(e, k):
        k0, width = KS[k]
        w2 = width // 2
        landed(zr[k].at[e], dr_sem.at[e, k])
        lhs[0:256, pl.ds(k0, w2)] = zr[k][e, :, 0:16, :].reshape(N * 16, w2)
        lhs[0:256, pl.ds(k0 + w2, w2)] = zr[k][e, :, 16:32, :].reshape(N * 16, w2)
        rem = zr[k][e, :, 32:40, :].reshape(N * 8, w2)
        lhs[256:320, pl.ds(k0, w2)] = dot(unfold_l, rem).astype(bf16)
        lhs[256:320, pl.ds(k0 + w2, w2)] = dot(unfold_r, rem).astype(bf16)

    def finish(f, gu):
        h[:, pl.ds(pl.multiple_of(f * FT, FT), FT)] = (jax.nn.silu(gu[:, :FT]) * gu[:, FT:]).astype(bf16)

    def sweep(e, ks, tile):
        def group(f0, n):
            gs = [e * NF + f0 + t for t in range(n)]
            for g in gs:
                for k in ks:
                    wb_wait(g, k)
            for t, g in enumerate(gs):
                tile(f0 + t, g % RING)
            for g in gs:
                @pl.when(g + RING < LOCAL * NF)
                def _():
                    for k in ks:
                        wb_start(g + RING, k)

        @pl.loop(0, NF // GROUP)
        def _(i):
            group(i * GROUP, GROUP)

        group(NF // GROUP * GROUP, NF % GROUP)

    def first(f, s):
        acc[f] = dot(lhs[:, pl.ds(*KS[0])], wb[s, pl.ds(*KS[0]), :])

    def second(f, s):
        finish(f, acc[f] + dot(lhs[:, pl.ds(*KS[1])], wb[s, pl.ds(*KS[1]), :]))

    def whole(f, s):
        finish(f, dot(lhs[...], wb[s]))

    for e in range(LOCAL):
        if e == 0:
            arrive(e, 0)
            sweep(e, (0,), first)
            arrive(e, 1)
            sweep(e, (1,), second)
        else:
            arrive(e, 0)
            arrive(e, 1)
            sweep(e, (0, 1), whole)

        for c, (c0, width) in enumerate(CHUNKS):
            w2 = width // 2
            wd_copy(e, c).wait()
            out = dot(h[...], wd[:, pl.ds(c0, width)])
            if e + 1 < LOCAL:
                wd_copy(e + 1, c).start()
            main = out[0:256].astype(bf16)
            os[c][e, :, 0:16, :] = main[:, :w2].reshape(N, 16, w2)
            os[c][e, :, 16:32, :] = main[:, w2:].reshape(N, 16, w2)
            rem = out[256:320].reshape(N, 4, width)
            os[c][e, :, 32:40, :] = jnp.concatenate([rem[:, :, :w2], rem[:, :, w2:]], axis=1).astype(bf16)
            for d in order:
                comb(e, c, d).start()
            cr[c][e, me] = os[c][e, me]

    for c, (c0, width) in enumerate(CHUNKS):
        w2 = width // 2
        for e in range(LOCAL):
            landed(cr[c].at[e], cr_sem.at[e, c])
        for side in range(2):
            total = 0
            for e in range(LOCAL):
                total += dot(bm[e], cr[c][e, :, 16 * side:16 * side + 16, :].reshape(N * 16, w2))
                total += dot(br[e, side], cr[c][e, :, 32:40, :].reshape(N * 8, w2))
            y_ref[:, pl.ds(c0 + side * w2, w2)] = total.astype(bf16)

    for e in range(LOCAL):
        for k in range(len(KS)):
            landed(zs[k].at[e], ds_sem.at[e, k])
        for c in range(len(CHUNKS)):
            landed(os[c].at[e], cs_sem.at[e, c])


def solution(mesh):
    def body(x, expert, slot, gate, wg, wu, wd):
        vmem = pl.BlockSpec(memory_space=pltpu.VMEM)
        hbm = pl.BlockSpec(memory_space=pltpu.HBM)
        halves = [w // 2 for _, w in CHUNKS]
        y = pl.pallas_call(
            kernel,
            name="moe",
            out_shape=jax.ShapeDtypeStruct((T, D), bf16),
            in_specs=[hbm, vmem, vmem, vmem, hbm, hbm, hbm],
            out_specs=vmem,
            scratch_shapes=[
                pltpu.VMEM((T, D), bf16),
                *[pltpu.VMEM((LOCAL, N, 40, w // 2), bf16) for _, w in KS],
                *[pltpu.VMEM((LOCAL, N, 40, w // 2), bf16) for _, w in KS],
                pltpu.VMEM((N * SLOTS, D), bf16),
                pltpu.VMEM((NF, N * SLOTS, 2 * FT), f32),
                pltpu.VMEM((N * SLOTS, F), bf16),
                pltpu.VMEM((RING, D, 2 * FT), bf16),
                pltpu.VMEM((F, D), bf16),
                *[pltpu.VMEM((LOCAL, N, 40, w), bf16) for w in halves],
                *[pltpu.VMEM((LOCAL, N, 40, w), bf16) for w in halves],
                pltpu.VMEM((LOCAL, T, N * MAIN), bf16),
                pltpu.VMEM((LOCAL, 2, T, N * 8), bf16),
                pltpu.SemaphoreType.DMA,
                pltpu.SemaphoreType.DMA((len(KS), RING)),
                pltpu.SemaphoreType.DMA((len(CHUNKS),)),
                pltpu.SemaphoreType.DMA((LOCAL, len(KS))),
                pltpu.SemaphoreType.DMA((LOCAL, len(KS))),
                pltpu.SemaphoreType.DMA((LOCAL, len(CHUNKS))),
                pltpu.SemaphoreType.DMA((LOCAL, len(CHUNKS))),
            ],
            compiler_params=pltpu.CompilerParams(
                collective_id=0, has_side_effects=True, vmem_limit_bytes=VMEM_LIMIT),
        )(x[0, 0], expert[0, 0].T, slot[0, 0].T, gate[0, 0].T, wg, wu, wd)
        return y[None, None]

    tok, weights = P("dp", "ep", None, None), P("ep", None, None)
    return jax.shard_map(body, mesh=mesh, in_specs=(tok,) * 4 + (weights,) * 3, out_specs=tok, check_vma=False)
```

time: 86.2 us -> 73.5 us (0.85)
  Pallas kernels: 79.3 us -> 71.1 us
  local copies, waits for them, and re-layouts: 6.58 us -> 2.16 us
    pallas_call x1, Pallas kernels: 79.3 us -> 71.1 us  [body(): pl.pallas_call(kernel, name='moe', out_shape=jax.ShapeDtypeStruct((T, D),...]
    unnamed x4 -> x1, local copies, waits for them, and re-layouts: 6.58 us -> 2.16 us
where the time goes in v2:
time: 73.5 us; the launch traced here: 73.3 us
  Pallas kernels  71.1 us (97%)
  local copies, waits for them, and re-layouts  2.16 us (3%)
    pallas_call x1, Pallas kernels, body(): pl.pallas_call(kernel, name='moe', out_shape=jax.ShapeDtypeStruct((T, D),...  71.1 us
    unnamed x1, local copies, waits for them, and re-layouts  2.16 us

profile of v2, /device:TPU:0, one launch (start us, length us, event | category | flops | bytes accessed | tf_op | source)
XLA Modules:
  0.0 73.3 jit_solution(13603285915990707797)
XLA Ops:
  0.0 71.1 %moe.1 = bf16[256,1792]{1,0:T(8,128)(2,1)} custom-call(bf16[256,1792]{1,0:T(8,128)(2,1)} %bitcast.12, s32[2,256]{1,0:T(2,128)} %bitcast.13, s32[2,256]{1,0:T(2,128)} %bitcast.14, f32[2,256]{1,0:T(2,128)} %bitcast.15, bf16[2,1792,4864]{2,1,0:T(8,128)(2,1)} %wg_hbm.1, bf16[2,1792,4864]{2,1,0:T(8,128)(2,1)} %wu_hbm.1, bf16[2,4864,1792]{2,1,0:T(8,128)(2,1)} %wd_hbm.1), custom_call_target="tpu_custom_call" | custom-call | tf_op jit(solution)/shard_map/moe/pallas_call | solution.py:231
  71.1 2.2 %copy.9 = bf16[1,1,256,1792]{3,2,1,0:T(8,128)(2,1)} copy(bf16[1,1,256,1792]{3,2,1,0:T(8,128)(2,1)} %bitcast.11) | data formatting | bytes 1835008

commit v3 on v0

v3 whole, which is shorter than its diff:
```python
import jax
import jax.numpy as jnp
from jax import lax
from jax.experimental import pallas as pl
from jax.experimental.pallas import tpu as pltpu
from jax.sharding import PartitionSpec as P

N = 16
LOCAL = 2
T, D, F = 256, 1792, 4864
SLOTS = 20
HALF = D // 2
FT = 256
NF = F // FT
RING, GROUP = 15, 5
AGAIN = NF - RING
assert AGAIN <= NF % GROUP
LOADS = NF + AGAIN
CHUNKS = ((0, 1024), (1024, 512), (1536, 256))
VMEM_LIMIT = 67_043_328
PART = ((0, 16), (16, 24))
SPAN = ((0, 128), (128, 192))
f32, bf16, i32 = jnp.float32, jnp.bfloat16, jnp.int32


def dot(a, b):
    return jnp.dot(a, b, preferred_element_type=f32)


def iota(shape, axis):
    return lax.broadcasted_iota(i32, shape, axis)


def code_of(r, e, side, rows, q0):
    d = {16: r >> 4, 24: (r * 2731) >> 16, 40: (r * 1639) >> 16}[rows]
    q = r - rows * d + q0
    early = q < 32
    half = jnp.where(early, (q >> 3) & 1, (q >> 2) & 1)
    place = jnp.where(early, ((q >> 4) << 3) + (q & 7), 16 + (q & 3))
    return jnp.where(half == side, (2 * d + e) * 32 + place, -2)


def kernel(x_hbm, expert, slot, gate, wg_hbm, wu_hbm, wd_hbm, y_hbm,
           x_v, zs0, zs1, zr0, zr1, lhs, h, wb, wd, os0, os1, os2, cr0, cr1, cr2, bl0, bl11, bl10, y_p,
           x_sem, y_sem, wb_sem, wd_sem, ds_sem, dr_sem, cs_sem, cr_sem):
    zs, zr = (zs0, zs1), (zr0, zr1)
    os, cr = (os0, os1, os2), (cr0, cr1, cr2)
    me = lax.axis_index("ep")
    bits = [(me // (1 << b)) % 2 for b in range(4)]

    def partner(k):
        return sum((1 - bits[b] if (k >> b) & 1 else bits[b]) * (1 << b) for b in range(4))

    order = [partner((7 * k) % 16) for k in range(1, N)]

    barrier = pltpu.get_barrier_semaphore()
    for d in order:
        pl.semaphore_signal(barrier, inc=1, device_id={"ep": d}, device_id_type=pl.DeviceIdType.MESH)
    x_copy = pltpu.make_async_copy(x_hbm, x_v, x_sem)
    x_copy.start()

    def wb_start(load):
        e, f, s = load // LOADS, load % LOADS % NF, load % RING
        cols = pl.ds(pl.multiple_of(f * FT, FT), FT)
        pltpu.make_async_copy(wg_hbm.at[e, :, cols], wb.at[s, :, pl.ds(0, FT)], wb_sem.at[s]).start()
        pltpu.make_async_copy(wu_hbm.at[e, :, cols], wb.at[s, :, pl.ds(FT, FT)], wb_sem.at[s]).start()

    def wb_wait(load):
        part = wb.at[load % RING]
        pltpu.make_async_copy(part, part, wb_sem.at[load % RING]).wait()

    def wd_copy(e, c):
        cols = pl.ds(*CHUNKS[c])
        return pltpu.make_async_copy(wd_hbm.at[e, :, cols], wd.at[:, cols], wd_sem.at[c])

    row = [jnp.where(slot[j:j + 1] < SLOTS, expert[j:j + 1] * 32 + slot[j:j + 1], -1) for j in range(2)]

    def pick(code):
        shape = (code.shape[0], T)
        hit = (jnp.broadcast_to(code, shape) == jnp.broadcast_to(row[0], shape)) | (
            jnp.broadcast_to(code, shape) == jnp.broadcast_to(row[1], shape))
        return jnp.where(hit, 1.0, 0.0).astype(bf16)

    def column(v):
        return jnp.transpose(jnp.broadcast_to(v, (128, T)))[:, 0:1]

    def disp(e, p, d):
        return pltpu.make_async_remote_copy(
            src_ref=zs[p].at[e, d], dst_ref=zr[p].at[e, me], send_sem=ds_sem.at[e, p], recv_sem=dr_sem.at[e, p],
            device_id={"ep": d}, device_id_type=pl.DeviceIdType.MESH)

    for e, p in ((0, 0), (0, 1), (1, 1), (1, 0)):
        q0, rows = PART[p]
        r = iota((N * rows, 1), 0)
        picks = [pick(code_of(r, e, side, rows, q0)) for side in range(2)]
        if (e, p) == (0, 0):
            x_copy.wait()
            for load in range(RING):
                wb_start(load)
        z = dot(picks[0], x_v[:, :HALF]) + dot(picks[1], x_v[:, HALF:])
        zs[p][e] = z.astype(bf16).reshape(N, rows, HALF)
        if (e, p) == (0, 0):
            pl.semaphore_wait(barrier, N - 1)
        for d in order:
            disp(e, p, d).start()
        zr[p][e, me] = zs[p][e, me]

    un_r = iota((64, 128), 0)
    un_c = iota((64, 128), 1)
    unfold = [jnp.where((un_r >> 2) * 8 + (un_r & 3) + 4 * side == un_c, 1.0, 0.0).astype(bf16) for side in range(2)]

    col = [column(row[j]) for j in range(2)]
    weight = [column(gate[j:j + 1].astype(bf16).astype(f32)) for j in range(2)]

    for ref, e, q0, rows in ((bl0, 0, 0, 40), (bl11, 1, *PART[1]), (bl10, 1, *PART[0])):
        for side in range(2):
            code = code_of(iota((1, N * rows), 1), e, side, rows, q0)
            shape = (T, N * rows)
            ref[side] = sum(jnp.where(jnp.broadcast_to(col[j], shape) == jnp.broadcast_to(code, shape),
                                      jnp.broadcast_to(weight[j], shape), 0.0) for j in range(2)).astype(bf16)

    def block_rows(e, p):
        return (0, pl.ds(0, 40)) if e == 0 else (1 + p, pl.ds(*PART[p]))

    def comb(e, p, c, d):
        i, rows = block_rows(e, p)
        return pltpu.make_async_remote_copy(
            src_ref=os[c].at[e, d, rows], dst_ref=cr[c].at[e, me, rows], send_sem=cs_sem.at[i, c],
            recv_sem=cr_sem.at[i, c], device_id={"ep": d}, device_id_type=pl.DeviceIdType.MESH)

    def landed(ref, sem):
        pltpu.make_async_copy(ref.at[pl.ds(0, N - 1)], ref.at[pl.ds(0, N - 1)], sem).wait()

    def arrive(e, p):
        m0 = SPAN[p][0]
        landed(zr[p].at[e], dr_sem.at[e, p])
        for side in range(2):
            cols = pl.ds(side * HALF, HALF)
            lhs[m0:m0 + 128, cols] = zr[p][e, :, 8 * side:8 * side + 8, :].reshape(N * 8, HALF)
            if p == 1:
                lhs[256:320, cols] = dot(unfold[side], zr[p][e, :, 16:24, :].reshape(N * 8, HALF)).astype(bf16)

    def sweep(e, p, again):
        first = e * LOADS + (AGAIN if again else 0)
        rows = pl.ds(*SPAN[p])

        def arrived(load0, n):
            for t in range(n):
                wb_wait(load0 + t)

        def multiply(load0, n):
            for t in range(n):
                load = load0 + t
                gu = dot(lhs[rows, :], wb[load % RING])
                f = load % LOADS % NF
                h[rows, pl.ds(pl.multiple_of(f * FT, FT), FT)] = (jax.nn.silu(gu[:, :FT]) * gu[:, FT:]).astype(bf16)

        def refill(load0, n):
            for t in range(n):
                wb_start(load0 + t + RING)

        if not again:
            arrived(first, GROUP)
        multiply(first, GROUP)
        refill(first, AGAIN)
        if again and e == 0:
            for c in range(1, len(CHUNKS)):
                wd_copy(0, c).start()

        @pl.loop(1, NF // GROUP)
        def _(i):
            load0 = first + i * GROUP
            if not again:
                arrived(load0, GROUP)
            multiply(load0, GROUP)
            if again and e + 1 < LOCAL:
                for t in range(GROUP):
                    load = load0 - GROUP + t

                    @pl.when(load >= first + AGAIN)
                    def _():
                        wb_start(load + RING)

        n = NF % GROUP
        load0 = first + NF - n
        arrived(load0 + n - AGAIN if again else load0, AGAIN if again else n)
        if not again:
            for c in range(1) if e == 0 else range(1, len(CHUNKS)):
                wd_copy(e, c).start()
        multiply(load0, n)
        if again and e + 1 < LOCAL:
            refill(load0 - GROUP, GROUP + n)

    def down(e, parts):
        m0, m1 = SPAN[parts[0]][0], sum(SPAN[parts[-1]])
        for c, (c0, width) in enumerate(CHUNKS):
            w2 = width // 2
            if parts[0] == 0 and e == 0 or parts[0] == 1:
                wd_copy(e, c).wait()
            if width == 256:
                k = 2560
                y_p[0:m1 - m0, 0:width] = dot(h[m0:m1, :k], wd[:k, pl.ds(c0, width)])
                out = y_p[0:m1 - m0, 0:width] + dot(h[m0:m1, k:], wd[k:, pl.ds(c0, width)])
            else:
                out = dot(h[m0:m1, :], wd[:, pl.ds(c0, width)])
            for p in parts:
                q0, base = PART[p][0], SPAN[p][0] - m0
                for side in range(2):
                    half = out[base:base + 128, side * w2:side * w2 + w2].astype(bf16)
                    os[c][e, :, q0 + 8 * side:q0 + 8 * side + 8, :] = half.reshape(N, 8, w2)
                if p == 1:
                    rem = out[base + 128:base + 192].reshape(N, 4, width)
                    os[c][e, :, 32:40, :] = jnp.concatenate([rem[:, :, :w2], rem[:, :, w2:]], axis=1).astype(bf16)
            for d in order:
                comb(e, parts[0], c, d).start()
            own = block_rows(e, parts[0])[1]
            cr[c][e, me, own] = os[c][e, me, own]
        if e + 1 < LOCAL:
            wd_copy(e + 1, 0).start()

    arrive(0, 0)
    sweep(0, 0, False)
    arrive(0, 1)
    sweep(0, 1, True)
    down(0, (0, 1))
    arrive(1, 1)
    sweep(1, 1, False)
    down(1, (1,))
    arrive(1, 0)
    sweep(1, 0, True)
    down(1, (0,))

    def y_copy(c):
        cols = pl.ds(*CHUNKS[c])
        return pltpu.make_async_copy(x_v.at[:, cols], y_hbm.at[:, cols], y_sem.at[c])

    late = pl.ds(*PART[0])

    def wait_for(e, p, c):
        i, rows = block_rows(e, p)
        landed(cr[c].at[e, :, rows], cr_sem.at[i, c])

    for c, (c0, width) in enumerate(CHUNKS):
        w2 = width // 2
        wait_for(0, 0, c)
        wait_for(1, 1, c)
        for side in range(2):
            y_p[0:T, pl.ds(c0 + side * w2, w2)] = dot(bl0[side], cr[c][0].reshape(N * 40, w2)) + dot(
                bl11[side], cr[c][1, :, pl.ds(*PART[1]), :].reshape(N * 24, w2))
    for c, (c0, width) in enumerate(CHUNKS):
        w2 = width // 2
        wait_for(1, 0, c)
        for side in range(2):
            cols = pl.ds(c0 + side * w2, w2)
            x_v[:, cols] = (y_p[0:T, cols] + dot(bl10[side], cr[c][1, :, late, :].reshape(N * 16, w2))).astype(bf16)
        y_copy(c).start()

    for e in range(LOCAL):
        for p in range(2):
            landed(zs[p].at[e], ds_sem.at[e, p])
    for c in range(len(CHUNKS)):
        for e, p in ((0, 0), (1, 1), (1, 0)):
            i, rows = block_rows(e, p)
            landed(os[c].at[e, :, rows], cs_sem.at[i, c])
        y_copy(c).wait()


def solution(mesh):
    def body(x, expert, slot, gate, wg, wu, wd):
        vmem = pl.BlockSpec(memory_space=pltpu.VMEM)
        hbm = pl.BlockSpec(memory_space=pltpu.HBM)
        halves = [w // 2 for _, w in CHUNKS]
        dma = pltpu.SemaphoreType.DMA
        y = pl.pallas_call(
            kernel,
            name="moe",
            out_shape=jax.ShapeDtypeStruct((T, D), bf16),
            in_specs=[hbm, vmem, vmem, vmem, hbm, hbm, hbm],
            out_specs=hbm,
            scratch_shapes=[
                pltpu.VMEM((T, D), bf16),
                *[pltpu.VMEM((LOCAL, N, rows, HALF), bf16) for _, rows in PART],
                *[pltpu.VMEM((LOCAL, N, rows, HALF), bf16) for _, rows in PART],
                pltpu.VMEM((N * SLOTS, D), bf16),
                pltpu.VMEM((N * SLOTS, F), bf16),
                pltpu.VMEM((RING, D, 2 * FT), bf16),
                pltpu.VMEM((F, D), bf16),
                *[pltpu.VMEM((LOCAL, N, 40, w), bf16) for w in halves],
                *[pltpu.VMEM((LOCAL, N, 40, w), bf16) for w in halves],
                *[pltpu.VMEM((2, T, N * rows), bf16) for rows in (40, 24, 16)],
                pltpu.VMEM((N * SLOTS, D), f32),
                dma,
                dma((len(CHUNKS),)),
                dma((RING,)),
                dma((len(CHUNKS),)),
                dma((LOCAL, 2)),
                dma((LOCAL, 2)),
                dma((3, len(CHUNKS))),
                dma((3, len(CHUNKS))),
            ],
            compiler_params=pltpu.CompilerParams(
                collective_id=0, has_side_effects=True, vmem_limit_bytes=VMEM_LIMIT),
        )(x[0, 0], expert[0, 0].T, slot[0, 0].T, gate[0, 0].T, wg, wu, wd)
        return y[None, None]

    tok, weights = P("dp", "ep", None, None), P("ep", None, None)
    return jax.shard_map(body, mesh=mesh, in_specs=(tok,) * 4 + (weights,) * 3, out_specs=tok, check_vma=False)
```

time: 171 us -> 67.1 us (0.39)
  matrix products: 84.2 us -> 0 us
  Pallas kernels: 0 us -> 64.7 us
  blocking collectives: 34.6 us -> 0 us
  waiting for transfers between devices: 26.7 us -> 0 us
  local copies, waits for them, and re-layouts: 22.2 us -> 2.16 us
  starting transfers between devices: 2.85 us -> 0 us
    dot_general x7 -> x0, matrix products: 84.2 us -> none  [einsum(): return jnp.einsum(form, a.astype(jnp.float32), b.astype(jnp.float32))]
    pallas_call x0 -> x1, Pallas kernels: none -> 64.7 us  [body(): pl.pallas_call(kernel, name='moe', out_shape=jax.ShapeDtypeStruct((T, D),...]
    another operation x1 -> x0, blocking collectives: 34.6 us -> none  [placed(): return lax.with_sharding_constraint(v, NamedSharding(mesh, P(*spec)))]
    another operation x1 -> x0, waiting for transfers between devices: 26.7 us -> none  [placed(): return lax.with_sharding_constraint(v, NamedSharding(mesh, P(*spec)))]
    another operation x4 -> x0, local copies, waits for them, and re-layouts: 14.8 us -> none  [placed(): return lax.with_sharding_constraint(v, NamedSharding(mesh, P(*spec)))]
    unnamed x15 -> x1, local copies, waits for them, and re-layouts: 5.53 us -> 2.16 us
    another operation x1 -> x0, starting transfers between devices: 2.85 us -> none  [placed(): return lax.with_sharding_constraint(v, NamedSharding(mesh, P(*spec)))]
    eq x2 -> x0, local copies, waits for them, and re-layouts: 1.72 us -> none  [the longest x1 0.89 us: step(): to_slot = jax.nn.one_hot(slot, slots, dtype=jnp.bfloat16)]
  transfers between devices with their start and end apart: 1 -> 0, of which waited for: 1 -> 0; matrix products, arithmetic and copies ran while one was open for 2% -> 0% of each run, Pallas kernels for 0% -> 0%
where the time goes in v3:
time: 67.1 us; the launch traced here: 66.9 us
  Pallas kernels  64.7 us (96%)
  local copies, waits for them, and re-layouts  2.16 us (3%)
    pallas_call x1, Pallas kernels, body(): pl.pallas_call(kernel, name='moe', out_shape=jax.ShapeDtypeStruct((T, D),...  64.7 us
    unnamed x1, local copies, waits for them, and re-layouts  2.16 us

profile of v3, /device:TPU:0, one launch (start us, length us, event | category | flops | bytes accessed | tf_op | source)
XLA Modules:
  0.0 66.9 jit_solution(11922757666329351127)
XLA Ops:
  0.0 64.7 %moe.1 = bf16[256,1792]{1,0:T(8,128)(2,1)} custom-call(bf16[256,1792]{1,0:T(8,128)(2,1)} %bitcast.12, s32[2,256]{1,0:T(2,128)} %bitcast.13, s32[2,256]{1,0:T(2,128)} %bitcast.14, f32[2,256]{1,0:T(2,128)} %bitcast.15, bf16[2,1792,4864]{2,1,0:T(8,128)(2,1)} %wg_hbm.1, bf16[2,1792,4864]{2,1,0:T(8,128)(2,1)} %wu_hbm.1, bf16[2,4864,1792]{2,1,0:T(8,128)(2,1)} %wd_hbm.1), custom_call_target="tpu_custom_call" | custom-call | tf_op jit(solution)/shard_map/moe/pallas_call | solution.py:274
  64.7 2.2 %copy.9 = bf16[1,1,256,1792]{3,2,1,0:T(8,128)(2,1)} copy(bf16[1,1,256,1792]{3,2,1,0:T(8,128)(2,1)} %bitcast.11) | data formatting | bytes 1835008

commit v4 on v3

--- a/solution.py
+++ b/solution.py
@@ -40,9 +40,9 @@
     return jnp.where(half == side, (2 * d + e) * 32 + place, -2)
 
 
-def kernel(x_hbm, expert, slot, gate, wg_hbm, wu_hbm, wd_hbm, y_hbm,
-           x_v, zs0, zs1, zr0, zr1, lhs, h, wb, wd, os0, os1, os2, cr0, cr1, cr2, bl0, bl11, bl10, y_p,
-           x_sem, y_sem, wb_sem, wd_sem, ds_sem, dr_sem, cs_sem, cr_sem):
+def kernel(x_hbm, expert_hbm, slot_hbm, gate_hbm, wg_hbm, wu_hbm, wd_hbm, y_hbm,
+           expert, slot, gate, x_v, zs0, zs1, zr0, zr1, lhs, h, wb, wd, os0, os1, os2, cr0, cr1, cr2, bl0, bl11, bl10, y_p,
+           in_sem, x_sem, y_sem, wb_sem, wd_sem, ds_sem, dr_sem, cs_sem, cr_sem):
     zs, zr = (zs0, zs1), (zr0, zr1)
     os, cr = (os0, os1, os2), (cr0, cr1, cr2)
     me = lax.axis_index("ep")
@@ -51,11 +51,15 @@
     def partner(k):
         return sum((1 - bits[b] if (k >> b) & 1 else bits[b]) * (1 << b) for b in range(4))
 
-    order = [partner((7 * k) % 16) for k in range(1, N)]
+    order = [partner(k) for k in (14, 6, 2, 12, 4, 10, 8, 15, 7, 3, 13, 5, 11, 9, 1)]
 
     barrier = pltpu.get_barrier_semaphore()
     for d in order:
         pl.semaphore_signal(barrier, inc=1, device_id={"ep": d}, device_id_type=pl.DeviceIdType.MESH)
+    small = [pltpu.make_async_copy(src, dst, in_sem.at[i]) for i, (src, dst) in enumerate(
+        ((expert_hbm, expert), (slot_hbm, slot), (gate_hbm, gate)))]
+    for copy in small:
+        copy.start()
     x_copy = pltpu.make_async_copy(x_hbm, x_v, x_sem)
     x_copy.start()
 
@@ -73,6 +77,8 @@
         cols = pl.ds(*CHUNKS[c])
         return pltpu.make_async_copy(wd_hbm.at[e, :, cols], wd.at[:, cols], wd_sem.at[c])
 
+    for copy in small:
+        copy.wait()
     row = [jnp.where(slot[j:j + 1] < SLOTS, expert[j:j + 1] * 32 + slot[j:j + 1], -1) for j in range(2)]
 
     def pick(code):
@@ -267,7 +273,6 @@
 
 def solution(mesh):
     def body(x, expert, slot, gate, wg, wu, wd):
-        vmem = pl.BlockSpec(memory_space=pltpu.VMEM)
         hbm = pl.BlockSpec(memory_space=pltpu.HBM)
         halves = [w // 2 for _, w in CHUNKS]
         dma = pltpu.SemaphoreType.DMA
@@ -275,9 +280,10 @@
             kernel,
             name="moe",
             out_shape=jax.ShapeDtypeStruct((T, D), bf16),
-            in_specs=[hbm, vmem, vmem, vmem, hbm, hbm, hbm],
+            in_specs=[hbm] * 7,
             out_specs=hbm,
             scratch_shapes=[
+                *[pltpu.VMEM((2, T), t) for t in (i32, i32, f32)],
                 pltpu.VMEM((T, D), bf16),
                 *[pltpu.VMEM((LOCAL, N, rows, HALF), bf16) for _, rows in PART],
                 *[pltpu.VMEM((LOCAL, N, rows, HALF), bf16) for _, rows in PART],
@@ -289,6 +295,7 @@
                 *[pltpu.VMEM((LOCAL, N, 40, w), bf16) for w in halves],
                 *[pltpu.VMEM((2, T, N * rows), bf16) for rows in (40, 24, 16)],
                 pltpu.VMEM((N * SLOTS, D), f32),
+                dma((3,)),
                 dma,
                 dma((len(CHUNKS),)),
                 dma((RING,)),

time: 67.1 us -> 66.4 us (0.990)
  no operation moved by 1% of the time
where the time goes in v4:
time: 66.4 us; the launch traced here: 66.3 us
  Pallas kernels  64.1 us (97%)
  local copies, waits for them, and re-layouts  2.16 us (3%)
    pallas_call x1, Pallas kernels, body(): pl.pallas_call(kernel, name='moe', out_shape=jax.ShapeDtypeStruct((T, D),...  64.1 us
    unnamed x1, local copies, waits for them, and re-layouts  2.16 us

profile of v4, /device:TPU:0, one launch (start us, length us, event | category | flops | bytes accessed | tf_op | source)
XLA Modules:
  0.0 66.3 jit_solution(13400616723059004387)
XLA Ops:
  0.0 64.1 %moe.1 = bf16[256,1792]{1,0:T(8,128)(2,1)} custom-call(bf16[256,1792]{1,0:T(8,128)(2,1)} %bitcast.12, s32[2,256]{1,0:T(2,128)} %bitcast.13, s32[2,256]{1,0:T(2,128)} %bitcast.14, f32[2,256]{1,0:T(2,128)} %bitcast.15, bf16[2,1792,4864]{2,1,0:T(8,128)(2,1)} %wg_hbm.1, bf16[2,1792,4864]{2,1,0:T(8,128)(2,1)} %wu_hbm.1, bf16[2,4864,1792]{2,1,0:T(8,128)(2,1)} %wd_hbm.1), custom_call_target="tpu_custom_call" | custom-call | tf_op jit(solution)/shard_map/moe/pallas_call | solution.py:279
  64.1 2.2 %copy.9 = bf16[1,1,256,1792]{3,2,1,0:T(8,128)(2,1)} copy(bf16[1,1,256,1792]{3,2,1,0:T(8,128)(2,1)} %bitcast.11) | data formatting | bytes 1835008
